TPU v7x, 256 devices: a whole 4x4x8 slice. The times are simulated.
256 devices in a mesh: grp: 8 (over y, core), node: 32 (over z, x).
Axes of the slice: x: 4, y: 4, z: 8, core: 2. Of those that a mesh axis runs over, the one named last changes fastest.
Arguments:
- excitation: float32 [128, 262144], P(None, ('grp', 'node')), may hold values from -6 to 6
- points: float32 [3, 262144], P(None, ('grp', 'node')), may hold values from -5 to 5
- near_mask: int32 [256, 2], P(('grp', 'node')), may hold values from 0 to 1, as said below
- bit_order: int32 [3], replicated, may hold values from 0 to 2, as said below
- compress: float32 [262144, 256], P(('grp', 'node')), may hold values from -0.1875 to 0.1875
- level_self: float32 [3, 65536, 256], P(None, ('grp', 'node')), may hold values from -0.25 to 0.25
- level_partner: float32 [3, 65536, 256], P(None, ('grp', 'node')), may hold values from -0.25 to 0.25
- expand: float32 [65536, 8192], P(('grp', 'node')), may hold values from -0.375 to 0.375
Outputs:
- field: float32 [128, 262144], P(None, ('grp', 'node'))
Inputs may be any that keep to these rules, and one draw needn't show every extreme that they name: near_mask[b, 0] is 0 when b is the first cluster of its group and near_mask[b, 1] is 0 when b is the last; otherwise each entry is 0 or 1. `bit_order`: the entries are distinct bits of a node index; each of 0 to 2 appears once.
All inputs are finite; a program needn't handle non-finite values.
Results may differ from a plain program's by a relative error of at most 0.0001.
Values sent between devices are 32-bit elements; how exact they have to be, the bound alone decides.
A program may use at most 64 MiB of HBM per device.

v0:
```python
import functools
import math

import jax
import jax.numpy as jnp
from jax import lax
from jax.sharding import PartitionSpec as P

HIGH = lax.Precision.HIGHEST
SOFTEN = 0.01


def partner(block, axis, apart):
    count = lax.axis_size(axis)
    route = []
    for low in range(count):
        high = low | 1 << apart
        if high != low and high < count:
            route += [(low, high), (high, low)]
    return lax.ppermute(block, axis, route)


def padded(cells, sides, width):
    for axis, dim in sides:
        count = lax.axis_size(axis)
        ends = count - 1
        head = lax.slice_in_dim(cells, 0, width, axis=dim)
        tail = lax.slice_in_dim(cells, cells.shape[dim] - width, cells.shape[dim], axis=dim)
        cells = jnp.concatenate(
            [
                lax.ppermute(tail, axis, [(i, (i + 1) % count) for i in range(ends)]),
                cells,
                lax.ppermute(head, axis, [((i + 1) % count, i) for i in range(ends)]),
            ],
            axis=dim,
        )
    return cells


def kernel_block(sources, targets):
    dist_sq = (sources[0][:, None] - targets[0][None, :]) ** 2
    dist_sq = dist_sq + (sources[1][:, None] - targets[1][None, :]) ** 2
    dist_sq = dist_sq + (sources[2][:, None] - targets[2][None, :]) ** 2
    return lax.rsqrt(dist_sq + SOFTEN) * (1.0 / math.sqrt(sources.shape[1]))


def partner_state(value, bit):
    return partner(value, "node", bit)


def shards(excitation, points, near_mask, bit_order, compress, level_self, level_partner, expand):
    width = excitation.shape[1]
    state = jnp.dot(excitation, compress, precision=HIGH)
    bit_count = lax.axis_size("node").bit_length() - 1
    branches = [functools.partial(partner_state, bit=bit) for bit in range(bit_count)]
    for level in range(level_self.shape[0]):
        own_part = jnp.dot(state, level_self[level], precision=HIGH)
        moved = lax.switch(bit_order[level], branches, state)
        state = own_part + jnp.dot(moved, level_partner[level], precision=HIGH)
    partial_far = jnp.dot(state, expand, precision=HIGH)
    far = lax.psum_scatter(partial_far, "grp", scatter_dimension=1, tiled=True)
    wide_x, wide_p = (
        padded(excitation, (("node", 1),), width),
        padded(points, (("node", 1),), width),
    )
    flags = near_mask[0].astype(jnp.float32)

    def near_term(which):
        src_x = wide_x[:, which * width : (which + 1) * width]
        src_p = wide_p[:, which * width : (which + 1) * width]
        return jnp.dot(src_x, kernel_block(src_p, points), precision=HIGH)

    near = near_term(1)
    near = near + flags[0] * near_term(0) + flags[1] * near_term(2)
    return far + near


def solution(mesh):
    return jax.shard_map(
        shards,
        mesh=mesh,
        in_specs=(
            P(None, ("grp", "node")),
            P(None, ("grp", "node")),
            P(("grp", "node"), None),
            P(),
            P(("grp", "node"), None),
            P(None, ("grp", "node"), None),
            P(None, ("grp", "node"), None),
            P(("grp", "node"), None),
        ),
        out_specs=P(None, ("grp", "node")),
        check_vma=False,
    )
```

profile of v0, /device:TPU:2, one launch (start us, length us, event | category | flops | bytes accessed | tf_op | source)
XLA Modules:
  0.0 103.6 jit_solution(8729340938941234200)
XLA Ops:
  6.5 1.4 %fusion.103 = (s32[1]{0:T(128)}, s32[1]{0:T(128)}, s32[1]{0:T(128)}) fusion(s32[3]{0:T(128)} %param.26), kind=kLoop, calls=%fused_computation.94 | loop fusion | bytes 24 | tf_op jit(solution)/shard_map/slice | solution.py:58
  7.9 1.7 %fusion.104 = f32[128,256]{1,0:T(8,128)S(1)} fusion(f32[128,1024]{1,0:T(8,128)} %param.23, f32[1024,256]{1,0:T(8,128)S(1)} %copy-done), kind=kOutput, calls=%fused_computation.95 | convolution fusion | flops 402653184 | bytes 1703936 | tf_op jit(solution)/shard_map/dot_general | solution.py:53
  11.5 5.4 %conditional.3 = (f32[128,256]{1,0:T(8,128)}) conditional(s32[]{:T(128)} %bitcast.1, f32[128,256]{1,0:T(8,128)S(1)} %fusion.104, f32[128,256]{1,0:T(8,128)S(1)} %fusion.104, f32[128,256]{1,0:T(8,128)S(1)} %fusion.104, f32[128,256]{1,0:T(8,128)S(1)} %fusion.104, f32[128,256]{1,0:T(8,128)S(1)} %fusion.104), branch_computations={%region_0.0_spmd, %region_1.0_spmd, %region_2.0_spmd, %region_3.0_... | conditional | bytes 524336 | solution.py:58
  11.5 2.3 %collective-permute-start = (f32[128,256]{1,0:T(8,128)S(1)}, f32[128,256]{1,0:T(8,128)}, u32[]{:S(2)}, u32[]{:S(2)}) collective-permute-start(f32[128,256]{1,0:T(8,128)S(1)} %param), channel_id=1, source_target_pairs={{0,1},{1,0},{2,3},{3,2},{4,5},{5,4},{6,7},{7,6},{8,9},{9,8},{10,11... | collective-permute-start | bytes 393224 | tf_op jit(solution)/shard_map/cond/branch_0_fun/ppermute | solution.py:20
  13.9 3.1 %collective-permute-done = f32[128,256]{1,0:T(8,128)} collective-permute-done((f32[128,256]{1,0:T(8,128)S(1)}, f32[128,256]{1,0:T(8,128)}, u32[]{:S(2)}, u32[]{:S(2)}) %collective-permute-start) | collective-permute-done | bytes 131104 | tf_op jit(solution)/shard_map/cond/branch_0_fun/ppermute | solution.py:20
  17.0 1.3 %convolution_add_fusion.2 = f32[128,256]{1,0:T(8,128)S(1)} fusion(f32[128,256]{1,0:T(8,128)S(1)} %fusion.85, f32[128,256]{1,0:T(8,128)} %get-tuple-element.52, f32[3,256,256]{2,1,0:T(8,128)} %param.29), kind=kOutput, calls=%fused_computation.68 | convolution fusion | flops 100696064 | bytes 655360 | tf_op jit(solution)/shard_map/dot_general | solution.py:59
  18.3 1.2 %fusion.82 = f32[128,256]{1,0:T(8,128)S(1)} fusion(f32[128,256]{1,0:T(8,128)S(1)} %convolution_add_fusion.2, f32[3,256,256]{2,1,0:T(8,128)} %param.28), kind=kOutput, calls=%fused_computation.73 | convolution fusion | flops 100663296 | bytes 524288 | tf_op jit(solution)/shard_map/dot_general | solution.py:57
  20.1 6.7 %conditional.4 = (f32[128,256]{1,0:T(8,128)}) conditional(s32[]{:T(128)} %bitcast.4, f32[128,256]{1,0:T(8,128)S(1)} %convolution_add_fusion.2, f32[128,256]{1,0:T(8,128)S(1)} %convolution_add_fusion.2, f32[128,256]{1,0:T(8,128)S(1)} %convolution_add_fusion.2, f32[128,256]{1,0:T(8,128)S(1)} %convolution_add_fusion.2, ...), branch_computations={%region_5.0_spmd, %region_6.0_spmd, %region_7.0_spmd, %region_8.0_... | conditional | bytes 524336 | solution.py:58
  20.2 2.2 %collective-permute-start.6 = (f32[128,256]{1,0:T(8,128)S(1)}, f32[128,256]{1,0:T(8,128)}, u32[]{:S(2)}, u32[]{:S(2)}) collective-permute-start(f32[128,256]{1,0:T(8,128)S(1)} %param.6), channel_id=1, source_target_pairs={{0,2},{2,0},{1,3},{3,1},{4,6},{6,4},{5,7},{7,5},{8,10},{10,8},{9,1... | collective-permute-start | bytes 393224 | tf_op jit(solution)/shard_map/cond/branch_1_fun/ppermute | solution.py:20
  22.4 4.5 %collective-permute-done.6 = f32[128,256]{1,0:T(8,128)} collective-permute-done((f32[128,256]{1,0:T(8,128)S(1)}, f32[128,256]{1,0:T(8,128)}, u32[]{:S(2)}, u32[]{:S(2)}) %collective-permute-start.6) | collective-permute-done | bytes 131104 | tf_op jit(solution)/shard_map/cond/branch_1_fun/ppermute | solution.py:20
  26.8 1.3 %convolution_add_fusion.1 = f32[128,256]{1,0:T(8,128)S(1)} fusion(f32[128,256]{1,0:T(8,128)S(1)} %fusion.82, f32[128,256]{1,0:T(8,128)} %get-tuple-element.53, f32[3,256,256]{2,1,0:T(8,128)} %param.29), kind=kOutput, calls=%fused_computation.67 | convolution fusion | flops 100696064 | bytes 655360 | tf_op jit(solution)/shard_map/dot_general | solution.py:59
  30.0 5.2 %conditional.5 = (f32[128,256]{1,0:T(8,128)}) conditional(s32[]{:T(128)} %bitcast.7, f32[128,256]{1,0:T(8,128)S(1)} %convolution_add_fusion.1, f32[128,256]{1,0:T(8,128)S(1)} %convolution_add_fusion.1, f32[128,256]{1,0:T(8,128)S(1)} %convolution_add_fusion.1, f32[128,256]{1,0:T(8,128)S(1)} %convolution_add_fusion.1, ...), branch_computations={%region_10.0_spmd, %region_11.0_spmd, %region_12.0_spmd, %region_1... | conditional | bytes 524336 | solution.py:58
  30.0 2.0 %collective-permute-start.12 = (f32[128,256]{1,0:T(8,128)S(1)}, f32[128,256]{1,0:T(8,128)}, u32[]{:S(2)}, u32[]{:S(2)}) collective-permute-start(f32[128,256]{1,0:T(8,128)S(1)} %param.12), channel_id=1, source_target_pairs={{0,4},{4,0},{1,5},{5,1},{2,6},{6,2},{3,7},{7,3},{8,12},{12,8},{9,1... | collective-permute-start | bytes 393224 | tf_op jit(solution)/shard_map/cond/branch_2_fun/ppermute | solution.py:20
  32.0 3.2 %collective-permute-done.12 = f32[128,256]{1,0:T(8,128)} collective-permute-done((f32[128,256]{1,0:T(8,128)S(1)}, f32[128,256]{1,0:T(8,128)}, u32[]{:S(2)}, u32[]{:S(2)}) %collective-permute-start.12) | collective-permute-done | bytes 131104 | tf_op jit(solution)/shard_map/cond/branch_2_fun/ppermute | solution.py:20
  35.2 1.3 %convolution_add_fusion = f32[128,256]{1,0:T(8,128)S(1)} fusion(f32[128,256]{1,0:T(8,128)S(1)} %fusion.79, f32[128,256]{1,0:T(8,128)} %get-tuple-element.54, f32[3,256,256]{2,1,0:T(8,128)} %param.29), kind=kOutput, calls=%fused_computation.66 | convolution fusion | flops 100696064 | bytes 655360 | tf_op jit(solution)/shard_map/dot_general | solution.py:59
  36.5 10.1 %fusion.105 = f32[128,8192]{1,0:T(8,128)} fusion(f32[128,256]{1,0:T(8,128)S(1)} %convolution_add_fusion, f32[256,8192]{1,0:T(8,128)} %param.30), kind=kOutput, calls=%fused_computation.96 | convolution fusion | flops 3221225472 | bytes 12713984 | tf_op jit(solution)/shard_map/dot_general | solution.py:60
  47.7 3.4 %collective-permute-start.16 = (f32[128,1024]{1,0:T(8,128)S(1)}, f32[128,1024]{1,0:T(8,128)S(1)}, u32[]{:S(2)}, u32[]{:S(2)}) collective-permute-start(f32[128,1024]{1,0:T(8,128)S(1)} %copy-done.1), channel_id=1, source_target_pairs={{0,1},{1,2},{2,3},{3,4},{4,5},{5,6},{6,7},{7,8},{8,9},{9,10},{10,1... | collective-permute-start | bytes 1572872 | tf_op jit(solution)/shard_map/ppermute | solution.py:31
  51.1 2.5 %collective-permute-start.18 = (f32[128,1024]{1,0:T(8,128)S(1)}, f32[128,1024]{1,0:T(8,128)S(1)}, u32[]{:S(2)}, u32[]{:S(2)}) collective-permute-start(f32[128,1024]{1,0:T(8,128)S(1)} %copy-done.1), channel_id=1, source_target_pairs={{1,0},{2,1},{3,2},{4,3},{5,4},{6,5},{7,6},{8,7},{9,8},{10,9},{11,1... | collective-permute-start | bytes 1572872 | tf_op jit(solution)/shard_map/ppermute | solution.py:33
  53.6 3.4 %collective-permute-start.15 = (f32[3,1024]{1,0:T(4,128)S(1)}, f32[3,1024]{1,0:T(4,128)S(1)}, u32[]{:S(2)}, u32[]{:S(2)}) collective-permute-start(f32[3,1024]{1,0:T(4,128)S(1)} %copy-done.2), channel_id=1, source_target_pairs={{0,1},{1,2},{2,3},{3,4},{4,5},{5,6},{6,7},{7,8},{8,9},{9,10},{10,1... | collective-permute-start | bytes 36872 | tf_op jit(solution)/shard_map/ppermute | solution.py:31
  56.9 2.5 %collective-permute-start.17 = (f32[3,1024]{1,0:T(4,128)S(1)}, f32[3,1024]{1,0:T(4,128)S(1)}, u32[]{:S(2)}, u32[]{:S(2)}) collective-permute-start(f32[3,1024]{1,0:T(4,128)S(1)} %copy-done.2), channel_id=1, source_target_pairs={{1,0},{2,1},{3,2},{4,3},{5,4},{6,5},{7,6},{8,7},{9,8},{10,9},{11,1... | collective-permute-start | bytes 36872 | tf_op jit(solution)/shard_map/ppermute | solution.py:33
  59.5 4.0 %fusion.24 = f32[1024,128]{0,1:T(8,128)S(1)} fusion(f32[128,1024]{1,0:T(8,128)S(1)} %copy-done.1, f32[1024]{0:T(1024)S(1)} %bitcast.52, f32[1024]{0:T(1024)S(1)} %bitcast.55, f32[1024]{0:T(1024)S(1)} %bitcast.49), kind=kOutput, calls=%fused_computation.24 | convolution fusion | flops 1621098496 | bytes 1060864 | tf_op jit(solution)/shard_map/dot_general | solution.py:71
  64.1 4.7 %fusion.75 = f32[1024,128]{0,1:T(8,128)S(1)} fusion(f32[1024,128]{0,1:T(8,128)S(1)} %fusion.24, f32[128,1024]{1,0:T(8,128)S(1)} %collective-permute-done.16, f32[1024]{0:T(1024)S(1)} %bitcast.62, f32[1024]{0:T(1024)S(1)} %bitcast.63, f32[1024]{0:T(1024)S(1)} %bitcast.61, f32[1024]{0:T(1024)S(1)} %bitcast.53, f32[1024]{0:T(1024)S(1)} %bitcast.56, ...), kind=kOutput, calls=%fused_computation.65 | convolution fusion | flops 1621360640 | bytes 1597444 | tf_op jit(solution)/shard_map/dot_general | solution.py:71
  68.8 21.6 %reduce-scatter.2.cloned.1.call-done = f32[128,1024]{1,0:T(8,128)} async-done(((f32[128,8192]{1,0:T(8,128)}), f32[128,1024]{1,0:T(8,128)}) %reduce-scatter.2.cloned.1.call-update) | async-done | bytes 524304 | tf_op jit(solution)/shard_map/reduce_scatter | solution.py:61
  90.3 6.5 %fusion.72 = f32[128,1024]{1,0:T(8,128)} fusion(f32[128,1024]{1,0:T(8,128)} %reduce-scatter.2.cloned.1.call-done, f32[1024,128]{0,1:T(8,128)S(1)} %fusion.75, f32[128,1024]{1,0:T(8,128)S(1)} %collective-permute-done.18, f32[1024]{0:T(1024)S(1)} %bitcast.59, f32[1024]{0:T(1024)S(1)} %bitcast.60, f32[1024]{0:T(1024)S(1)} %bitcast.58, f32[1024]{0:T(1024)S(1)} %bitcast.54, ...), kind=kOutput, calls=%fused_computation.64 | convolution fusion | flops 1621491712 | bytes 2121732 | tf_op jit(solution)/shard_map/dot_general | solution.py:71
  (21 shorter events, 4.2 us)
Async XLA Ops:
  6.5 1.4 %copy-start = (f32[1024,256]{1,0:T(8,128)S(1)}, f32[1024,256]{1,0:T(8,128)}, u32[]{:S(2)}) copy-start(f32[1024,256]{1,0:T(8,128)} %param.27) | copy-start | bytes 3145732
  6.5 83.8 %reduce-scatter.2.cloned.1.call-start = ((), (), s32[]{:S(2)}) async-start(), calls=%async_computation.1 | async-start | bytes 4718592 | tf_op jit(solution)/shard_map/reduce_scatter | solution.py:61
  11.5 5.4 %collective-permute-start = (f32[128,256]{1,0:T(8,128)S(1)}, f32[128,256]{1,0:T(8,128)}, u32[]{:S(2)}, u32[]{:S(2)}) collective-permute-start(f32[128,256]{1,0:T(8,128)S(1)} %param), channel_id=1, source_target_pairs={{0,1},{1,0},{2,3},{3,2},{4,5},{5,4},{6,7},{7,6},{8,9},{9,8},{10,11... | collective-permute-start | bytes 393224 | tf_op jit(solution)/shard_map/cond/branch_0_fun/ppermute | solution.py:20
  20.2 6.7 %collective-permute-start.6 = (f32[128,256]{1,0:T(8,128)S(1)}, f32[128,256]{1,0:T(8,128)}, u32[]{:S(2)}, u32[]{:S(2)}) collective-permute-start(f32[128,256]{1,0:T(8,128)S(1)} %param.6), channel_id=1, source_target_pairs={{0,2},{2,0},{1,3},{3,1},{4,6},{6,4},{5,7},{7,5},{8,10},{10,8},{9,1... | collective-permute-start | bytes 393224 | tf_op jit(solution)/shard_map/cond/branch_1_fun/ppermute | solution.py:20
  30.0 5.2 %collective-permute-start.12 = (f32[128,256]{1,0:T(8,128)S(1)}, f32[128,256]{1,0:T(8,128)}, u32[]{:S(2)}, u32[]{:S(2)}) collective-permute-start(f32[128,256]{1,0:T(8,128)S(1)} %param.12), channel_id=1, source_target_pairs={{0,4},{4,0},{1,5},{5,1},{2,6},{6,2},{3,7},{7,3},{8,12},{12,8},{9,1... | collective-permute-start | bytes 393224 | tf_op jit(solution)/shard_map/cond/branch_2_fun/ppermute | solution.py:20
  46.6 1.0 %copy-start.1 = (f32[128,1024]{1,0:T(8,128)S(1)}, f32[128,1024]{1,0:T(8,128)}, u32[]{:S(2)}) copy-start(f32[128,1024]{1,0:T(8,128)} %param.23) | copy-start | bytes 1572868
  46.6 6.9 %copy-start.2 = (f32[3,1024]{1,0:T(4,128)S(1)}, f32[3,1024]{1,0:T(4,128)}, u32[]{:S(2)}) copy-start(f32[3,1024]{1,0:T(4,128)} %param.24) | copy-start | bytes 36868
  46.6 12.8 %copy-start.3 = (s32[1,2]{1,0:T(1,128)S(1)}, s32[1,2]{1,0:T(1,128)}, u32[]{:S(2)}) copy-start(s32[1,2]{1,0:T(1,128)} %param.25) | copy-start | bytes 28
  47.7 16.4 %collective-permute-start.16 = (f32[128,1024]{1,0:T(8,128)S(1)}, f32[128,1024]{1,0:T(8,128)S(1)}, u32[]{:S(2)}, u32[]{:S(2)}) collective-permute-start(f32[128,1024]{1,0:T(8,128)S(1)} %copy-done.1), channel_id=1, source_target_pairs={{0,1},{1,2},{2,3},{3,4},{4,5},{5,6},{6,7},{7,8},{8,9},{9,10},{10,1... | collective-permute-start | bytes 1572872 | tf_op jit(solution)/shard_map/ppermute | solution.py:31
  51.1 17.7 %collective-permute-start.18 = (f32[128,1024]{1,0:T(8,128)S(1)}, f32[128,1024]{1,0:T(8,128)S(1)}, u32[]{:S(2)}, u32[]{:S(2)}) collective-permute-start(f32[128,1024]{1,0:T(8,128)S(1)} %copy-done.1), channel_id=1, source_target_pairs={{1,0},{2,1},{3,2},{4,3},{5,4},{6,5},{7,6},{8,7},{9,8},{10,9},{11,1... | collective-permute-start | bytes 1572872 | tf_op jit(solution)/shard_map/ppermute | solution.py:33
  53.6 10.5 %collective-permute-start.15 = (f32[3,1024]{1,0:T(4,128)S(1)}, f32[3,1024]{1,0:T(4,128)S(1)}, u32[]{:S(2)}, u32[]{:S(2)}) collective-permute-start(f32[3,1024]{1,0:T(4,128)S(1)} %copy-done.2), channel_id=1, source_target_pairs={{0,1},{1,2},{2,3},{3,4},{4,5},{5,6},{6,7},{7,8},{8,9},{9,10},{10,1... | collective-permute-start | bytes 36872 | tf_op jit(solution)/shard_map/ppermute | solution.py:31
  56.9 7.1 %collective-permute-start.17 = (f32[3,1024]{1,0:T(4,128)S(1)}, f32[3,1024]{1,0:T(4,128)S(1)}, u32[]{:S(2)}, u32[]{:S(2)}) collective-permute-start(f32[3,1024]{1,0:T(4,128)S(1)} %copy-done.2), channel_id=1, source_target_pairs={{1,0},{2,1},{3,2},{4,3},{5,4},{6,5},{7,6},{8,7},{9,8},{10,9},{11,1... | collective-permute-start | bytes 36872 | tf_op jit(solution)/shard_map/ppermute | solution.py:33
Sparse Core Ops, SparseCore 0:
  46.8 43.4 reduce-scatter.1
where the time goes:
time: 104 us
  matrix products  34.5 us (33%)
  waiting for transfers between devices  32.3 us (31%)
  starting transfers between devices  18.2 us (18%)
  between operations  15.5 us (15%)
  local copies, waits for them, and re-layouts  3.04 us (3%)
    reduce_scatter x1, waiting for transfers between devices, shards(): far = lax.psum_scatter(partial_far, 'grp', scatter_dimension=1, tiled=True)  21.6 us
    dot_general x3, matrix products, near_term(): return jnp.dot(src_x, kernel_block(src_p, points), precision=HIGH)  15.1 us
    ppermute x3, waiting for transfers between devices, partner(): return lax.ppermute(block, axis, route)  10.7 us
    dot_general x1, matrix products, shards(): partial_far = jnp.dot(state, expand, precision=HIGH)  10.1 us
    ppermute x2, starting transfers between devices, padded(): lax.ppermute(tail, axis, [(i, (i + 1) % count) for i in range(ends)])  6.76 us
    ppermute x3, starting transfers between devices, partner(): return lax.ppermute(block, axis, route)  6.54 us
    ppermute x2, starting transfers between devices, padded(): lax.ppermute(head, axis, [((i + 1) % count, i) for i in range(ends)])  4.94 us
    dot_general x3, matrix products, shards(): state = own_part + jnp.dot(moved, level_partner[level], precision=HIGH)  3.9 us
  transfers between devices with their start and end apart: 8, of which 4 were waited for; matrix products, arithmetic and copies ran while one was open for 9% of the time, Pallas kernels for 0%

commit v1 on v0

v1 whole, which is shorter than its diff:
```python
import functools
import itertools

import jax
import jax.numpy as jnp
from jax import lax
from jax.experimental import pallas as pl
from jax.experimental.pallas import tpu as pltpu
from jax.sharding import PartitionSpec as P

F32 = jnp.float32
BF16 = jnp.bfloat16
MESH = pl.DeviceIdType.MESH
SOFTEN = 0.01

PARTS = 4
AWAY = (2, 3, 1, 0)


def split(value):
    high = value.astype(BF16)
    return high, (value - high.astype(F32)).astype(BF16)


def product(left, right_high, right_low):
    rows = left.shape[0] // 2
    both = jnp.dot(left, right_high, preferred_element_type=F32)
    rest = jnp.dot(left[:rows], right_low, preferred_element_type=F32)
    return both[:rows] + both[rows:] + rest


def stacked(value):
    return jnp.concatenate(split(value), axis=0)


def remote(source, target, sends, receives, device):
    return pltpu.make_async_remote_copy(
        src_ref=source,
        dst_ref=target,
        send_sem=sends,
        recv_sem=receives,
        device_id=device,
        device_id_type=MESH,
    )


def kernel(
    bits,
    sizes,
    x_hbm,
    points_hbm,
    mask,
    compress_hbm,
    self_hbm,
    partner_hbm,
    expand_hbm,
    out_hbm,
    x,
    points,
    columns,
    compress,
    weights,
    weights_high,
    weights_low,
    expand,
    expand_high,
    expand_low,
    g_high,
    g_low,
    x_both,
    near,
    state,
    moved,
    peer_state,
    share,
    first,
    straight,
    relayed,
    out,
    load_sem,
    expand_sem,
    out_sem,
    level_sems,
    peer_sems,
    peer_expand_sems,
    points_sems,
    x_sems,
    first_sems,
    straight_sems,
    relayed_sems,
):
    n_grp, n_node = sizes
    levels = len(bits)
    cols, block = x_hbm.shape
    rank = compress_hbm.shape[1]
    part = cols // PARTS
    half = block // 2
    ring = n_grp // 2

    grp, node = lax.axis_index("grp"), lax.axis_index("node")
    y, core = lax.div(grp, 2), lax.rem(grp, 2)

    def along(step):
        return (lax.rem(y + step, ring) * 2 + core, node)

    up, down = along(1), along(ring - 1)
    peer = (grp + 1 - 2 * core, node)
    after = (grp, lax.rem(node + 1, n_node))
    before = (grp, lax.rem(node + n_node - 1, n_node))

    def partner(bit):
        apart = 1 << bit
        return (grp, node + apart * (1 - 2 * lax.rem(lax.div(node, apart), 2)))

    partners = [partner(bit) for bit in bits]

    loads = [
        pltpu.make_async_copy(x_hbm, x.at[0], load_sem.at[0]),
        pltpu.make_async_copy(compress_hbm, compress, load_sem.at[1]),
        pltpu.make_async_copy(points_hbm, points.at[0], load_sem.at[2]),
        pltpu.make_async_copy(self_hbm, weights.at[0], load_sem.at[3]),
        pltpu.make_async_copy(partner_hbm, weights.at[1], load_sem.at[4]),
    ]
    for load in loads:
        load.start()

    barrier = pltpu.get_barrier_semaphore()
    everyone = partners + [peer, up, down, before, after]
    for device in everyone:
        pl.semaphore_signal(barrier, inc=1, device_id=device, device_id_type=MESH)

    def expand_columns(slot, of_core):
        target = lax.rem(y + AWAY[slot], ring) * 2 + of_core
        return expand_hbm.at[:, pl.ds(pl.multiple_of(target * block, block), block)]

    own_expand = [
        pltpu.make_async_copy(expand_columns(slot, core), expand.at[slot, 0], expand_sem.at[slot])
        for slot in range(ring)
    ]
    for copy in own_expand:
        copy.start()

    loads[0].wait()
    x_both[0] = stacked(x[0])
    loads[1].wait()
    state[0] = product(x_both[0], *split(compress[...]))

    pl.semaphore_wait(barrier, len(everyone))

    def level_copy(level, chunk):
        rows = pl.ds(pl.multiple_of(chunk * part, part), part)
        return remote(
            state.at[level, rows],
            moved.at[level, rows],
            level_sems.at[0, level, chunk],
            level_sems.at[1, level, chunk],
            partners[level],
        )

    for chunk in range(PARTS):
        level_copy(0, chunk).start()

    loads[2].wait()
    to_after = remote(points.at[0], points.at[1], points_sems.at[0, 0], points_sems.at[1, 0], after)
    to_before = remote(points.at[0], points.at[2], points_sems.at[0, 1], points_sems.at[1, 1], before)
    to_after.start()
    to_before.start()

    peer_expand = [
        remote(
            expand_columns(slot, 1 - core),
            expand.at[slot, 1],
            peer_expand_sems.at[0, slot],
            peer_expand_sems.at[1, slot],
            peer,
        )
        for slot in range(ring)
    ]
    for copy in peer_expand:
        copy.start()

    for which in range(2):
        loads[3 + which].wait()
    for level in range(levels):
        for which in range(2):
            high, low = split(weights[which, level])
            weights_high[which, level] = high
            weights_low[which, level] = low

    def turn(which):
        padded = jnp.concatenate([points[which] * 32.0, jnp.zeros((5, block), F32)], axis=0)
        columns[pl.ds(which * block, block), :] = padded.T

    tall = 16
    wide = block // tall

    def g_rows(index):
        rows = pl.ds(pl.multiple_of(index * tall, tall), tall)
        total = None
        for axis in range(3):
            apart = columns[rows, axis : axis + 1] - points[0, axis : axis + 1, :] * 32.0
            total = apart * apart if total is None else total + apart * apart
        high, low = split(lax.rsqrt(total + SOFTEN * 1024.0))
        g_high[rows, :] = high
        g_low[rows, :] = low

    def g_span(low, high):
        def body(index, carry):
            g_rows(index)
            return carry

        lax.fori_loop(low, high, body, 0)

    turn(0)
    g_span(0, wide)

    def level_step(level, chunk):
        rows = pl.ds(pl.multiple_of(chunk * part, part), part)
        own = product(stacked(state[level, rows]), weights_high[0, level], weights_low[0, level])
        level_copy(level, chunk).wait_recv()
        came = product(stacked(moved[level, rows]), weights_high[1, level], weights_low[1, level])
        state[level + 1, rows] = own + came

    for level in range(levels - 1):

        def level_body(chunk, carry, level=level):
            level_step(level, chunk)
            level_copy(level + 1, chunk).start()
            return carry

        lax.fori_loop(0, PARTS, level_body, 0)
        if level == 0:
            to_after.wait_recv()
            to_before.wait_recv()
            turn(1)
            turn(2)

    x_after = remote(x.at[0], x.at[1], x_sems.at[0, 0], x_sems.at[1, 0], after)
    x_before = remote(x.at[0], x.at[2], x_sems.at[0, 1], x_sems.at[1, 1], before)
    x_after.start()
    x_before.start()

    for slot in range(ring):
        own_expand[slot].wait()
        peer_expand[slot].wait_recv()

        def convert(index, carry, slot=slot):
            rows = pl.ds(pl.multiple_of(index * 32, 32), 32)
            for which in range(2):
                high, low = split(expand[slot, which, rows, :])
                expand_high[slot, which, rows, :] = high
                expand_low[slot, which, rows, :] = low
            return carry

        lax.fori_loop(0, rank // 32, convert, 0)

    def peer_copy(chunk):
        rows = pl.ds(pl.multiple_of(chunk * part, part), part)
        return remote(
            state.at[levels, rows],
            peer_state.at[rows],
            peer_sems.at[0, chunk],
            peer_sems.at[1, chunk],
            peer,
        )

    def first_copy(chunk, side):
        return remote(
            share.at[chunk, 0, side],
            first.at[chunk, side],
            first_sems.at[0, chunk, side],
            first_sems.at[1, chunk, side],
            (down, up)[side],
        )

    def straight_copy(chunk, side):
        return remote(
            share.at[chunk, 1 + side, 1 - side],
            straight.at[chunk, side],
            straight_sems.at[0, chunk, side],
            straight_sems.at[1, chunk, side],
            (down, up)[side],
        )

    def relayed_copy(chunk, side):
        return remote(
            share.at[chunk, 1 + side, side],
            relayed.at[chunk, side],
            relayed_sems.at[0, chunk, side],
            relayed_sems.at[1, chunk, side],
            (down, up)[side],
        )

    def far_step(chunk):
        rows = pl.ds(pl.multiple_of(chunk * part, part), part)
        own = stacked(state[levels, rows])
        peer_copy(chunk).wait_recv()
        other = stacked(peer_state[rows])
        for slot in range(ring):
            for side in range(2):
                span = pl.ds(side * half, half)
                share[chunk, slot, side] = product(
                    own, expand_high[slot, 0, :, span], expand_low[slot, 0, :, span]
                ) + product(other, expand_high[slot, 1, :, span], expand_low[slot, 1, :, span])
            if slot == 0:
                first_copy(chunk, 0).start()
                first_copy(chunk, 1).start()
            if slot == 1:
                straight_copy(chunk, 0).start()
            if slot == 2:
                straight_copy(chunk, 1).start()

    def relay_step(chunk):
        for side in range(2):
            first_copy(chunk, side).wait_recv()
            share[chunk, 1 + side, side] = share[chunk, 1 + side, side] + first[chunk, side]
            relayed_copy(chunk, side).start()

    turns = PARTS + 2
    each = -(-2 * wide // turns)

    def main_body(step, carry):
        @pl.when(step < PARTS)
        def _():
            level_step(levels - 1, step)
            peer_copy(step).start()

        @pl.when(jnp.logical_and(step >= 1, step < PARTS + 1))
        def _():
            far_step(step - 1)

        @pl.when(step >= 2)
        def _():
            relay_step(step - 2)

        g_span(wide + step * each, jnp.minimum(wide + (step + 1) * each, 3 * wide))
        return carry

    lax.fori_loop(0, turns, main_body, 0)

    for which in range(3):
        if which == 1:
            x_after.wait_recv()
        if which == 2:
            x_before.wait_recv()
        if which:
            x_both[which] = stacked(x[which] * mask[0, which - 1].astype(F32))

        def near_body(index, carry, which=which):
            span = pl.ds(pl.multiple_of(index * 256, 256), 256)
            rows = pl.ds(which * block, block)
            term = product(x_both[which], g_high[rows, span], g_low[rows, span])
            near[:, span] = term if which == 0 else near[:, span] + term
            return carry

        lax.fori_loop(0, block // 256, near_body, 0)

    def out_copy(chunk):
        rows = pl.ds(pl.multiple_of(chunk * part, part), part)
        return pltpu.make_async_copy(out.at[rows], out_hbm.at[rows], out_sem.at[chunk])

    def final_body(chunk, carry):
        rows = pl.ds(pl.multiple_of(chunk * part, part), part)
        for side in range(2):
            straight_copy(chunk, 1 - side).wait_recv()
            relayed_copy(chunk, side).wait_recv()
            span = pl.ds(side * half, half)
            out[rows, span] = (
                near[rows, span]
                + share[chunk, 3, side]
                + straight[chunk, 1 - side]
                + relayed[chunk, side]
            )
        out_copy(chunk).start()
        return carry

    lax.fori_loop(0, PARTS, final_body, 0)

    def drain(chunk, carry):
        for level in range(levels):
            level_copy(level, chunk).wait_send()
        peer_copy(chunk).wait_send()
        for side in range(2):
            first_copy(chunk, side).wait_send()
            straight_copy(chunk, side).wait_send()
            relayed_copy(chunk, side).wait_send()
        out_copy(chunk).wait()
        return carry

    lax.fori_loop(0, PARTS, drain, 0)
    for copy in [to_after, to_before, x_after, x_before] + peer_expand:
        copy.wait_send()


def solution(mesh):
    sizes = (mesh.shape["grp"], mesh.shape["node"])

    def shards(excitation, points, near_mask, bit_order, compress, level_self, level_partner, expand):
        cols, block = excitation.shape
        rank = compress.shape[1]
        levels = level_self.shape[0]
        part = cols // PARTS
        half = block // 2
        ring = sizes[0] // 2
        hbm = pl.BlockSpec(memory_space=pltpu.HBM)
        dma = pltpu.SemaphoreType.DMA

        def call(bits, number):
            return pl.pallas_call(
                functools.partial(kernel, bits, sizes),
                out_shape=jax.ShapeDtypeStruct((cols, block), F32),
                in_specs=[hbm, hbm, pl.BlockSpec(memory_space=pltpu.SMEM), hbm, hbm, hbm, hbm],
                out_specs=hbm,
                scratch_shapes=[
                    pltpu.VMEM((3, cols, block), F32),
                    pltpu.VMEM((3, 3, block), F32),
                    pltpu.VMEM((3 * block, 8), F32),
                    pltpu.VMEM((block, rank), F32),
                    pltpu.VMEM((2, levels, rank, rank), F32),
                    pltpu.VMEM((2, levels, rank, rank), BF16),
                    pltpu.VMEM((2, levels, rank, rank), BF16),
                    pltpu.VMEM((ring, 2, rank, block), F32),
                    pltpu.VMEM((ring, 2, rank, block), BF16),
                    pltpu.VMEM((ring, 2, rank, block), BF16),
                    pltpu.VMEM((3 * block, block), BF16),
                    pltpu.VMEM((3 * block, block), BF16),
                    pltpu.VMEM((3, 2 * cols, block), BF16),
                    pltpu.VMEM((cols, block), F32),
                    pltpu.VMEM((levels + 1, cols, rank), F32),
                    pltpu.VMEM((levels, cols, rank), F32),
                    pltpu.VMEM((cols, rank), F32),
                    pltpu.VMEM((PARTS, ring, 2, part, half), F32),
                    pltpu.VMEM((PARTS, 2, part, half), F32),
                    pltpu.VMEM((PARTS, 2, part, half), F32),
                    pltpu.VMEM((PARTS, 2, part, half), F32),
                    pltpu.VMEM((cols, block), F32),
                    dma((5,)),
                    dma((ring,)),
                    dma((PARTS,)),
                    dma((2, levels, PARTS)),
                    dma((2, PARTS)),
                    dma((2, ring)),
                    dma((2, 2)),
                    dma((2, 2)),
                    dma((2, PARTS, 2)),
                    dma((2, PARTS, 2)),
                    dma((2, PARTS, 2)),
                ],
                compiler_params=pltpu.CompilerParams(
                    collective_id=number, has_side_effects=True, vmem_limit_bytes=62 << 20
                ),
                name=f"far_near_{number}",
            )

        orders = list(itertools.permutations(range(levels)))
        branches = [call(bits, number) for number, bits in enumerate(orders)]
        which = bit_order[0] * 2 + (bit_order[1] > bit_order[2]).astype(jnp.int32)
        return lax.switch(
            which,
            branches,
            excitation,
            points,
            near_mask,
            compress,
            level_self,
            level_partner,
            expand,
        )

    return jax.shard_map(
        shards,
        mesh=mesh,
        in_specs=(
            P(None, ("grp", "node")),
            P(None, ("grp", "node")),
            P(("grp", "node"), None),
            P(),
            P(("grp", "node"), None),
            P(None, ("grp", "node"), None),
            P(None, ("grp", "node"), None),
            P(("grp", "node"), None),
        ),
        out_specs=P(None, ("grp", "node")),
        check_vma=False,
    )
```

time: 104 us -> 58.5 us (0.56)
  Pallas kernels: 0 us -> 53.6 us
  matrix products: 34.5 us -> 0 us
  waiting for transfers between devices: 32.3 us -> 0 us
  starting transfers between devices: 18.2 us -> 0 us
  between operations: 15.5 us -> 1.91 us
    pallas_call x0 -> x1, Pallas kernels: none -> 53.6 us  [shards(): lax.switch(which, branches, excitation, points, near_mask, compress, leve...]
    dot_general x11 -> x0, matrix products: 34.5 us -> none  [the longest x3 15.1 us: near_term(): return jnp.dot(src_x, kernel_block(src_p, points), precision=HIGH)]
    reduce_scatter x1 -> x0, waiting for transfers between devices: 21.6 us -> none  [shards(): far = lax.psum_scatter(partial_far, 'grp', scatter_dimension=1, tiled=True)]
    ppermute x7 -> x0, starting transfers between devices: 18.2 us -> none  [the longest x2 6.76 us: padded(): lax.ppermute(tail, axis, [(i, (i + 1) % count) for i in range(ends)])]
    ppermute x7 -> x0, waiting for transfers between devices: 10.7 us -> none  [the longest x3 10.7 us: partner(): return lax.ppermute(block, axis, route)]
  transfers between devices with their start and end apart: 8 -> 0, of which waited for: 4 -> 0; matrix products, arithmetic and copies ran while one was open for 9% -> 0% of each run, Pallas kernels for 0% -> 0%
where the time goes in v1:
time: 58.5 us; the launch traced here: 58.1 us
  Pallas kernels  53.6 us (92%)
  local copies, waits for them, and re-layouts  2.18 us (4%)
  between operations  1.91 us (3%)
    pallas_call x1, Pallas kernels, shards(): lax.switch(which, branches, excitation, points, near_mask, compress, leve...  53.6 us
    slice x1, local copies, waits for them, and re-layouts, shards(): which = bit_order[0] * 2 + (bit_order[1] > bit_order[2]).astype(jnp.int32)  1.38 us

profile of v1, /device:TPU:2, one launch (start us, length us, event | category | flops | bytes accessed | tf_op | source)
XLA Modules:
  0.0 58.1 jit_solution(1736759370247504836)
XLA Ops:
  0.0 1.4 %fusion = (s32[1]{0:T(128)}, s32[1]{0:T(128)}, s32[1]{0:T(128)}) fusion(s32[3]{0:T(128)} %param.17), kind=kLoop, calls=%fused_computation | loop fusion | bytes 24 | tf_op jit(solution)/shard_map/slice | solution.py:457
  3.3 54.0 %conditional.1 = (f32[128,1024]{1,0:T(8,128)S(1)}) conditional(s32[]{:T(128)} %bitcast, (f32[128,1024]{1,0:T(8,128)}, f32[3,1024]{1,0:T(4,128)}, s32[1,2]{1,0:T(1,128)}, f32[1024,256]{1,0:T(8,128)}, f32[3,256,256]{2,1,0:T(8,128)}, /*index=5*/f32[3,256,256]{2,1,0:T(8,128)}, f32[256,8192]{1,0:T(8,128)}) %tuple.23, ...), branch_computations={%region_0.0_spmd, %region_1.0_spmd, %region_2.0_spmd, %region_3.0_... | conditional | bytes 8 | solution.py:458
  3.5 53.6 %far_near_4.1 = f32[128,1024]{1,0:T(8,128)S(1)} custom-call(f32[128,1024]{1,0:T(8,128)} %get-tuple-element.124.x_hbm, f32[3,1024]{1,0:T(4,128)} %get-tuple-element.125.points_hbm, s32[1,2]{1,0:T(1,128)} %get-tuple-element.126.mask, f32[1024,256]{1,0:T(8,128)} %get-tuple-element.127.compress_hbm, f32[3,256,256]{2,1,0:T(8,128)} %get-tuple-element.128.self_hbm, ...), custom_call_target="tpu_custom_call" | custom-call | tf_op jit(solution)/shard_map/cond/branch_4_fun/far_near_4/pallas_call | solution.py:458
  57.3 0.8 %copy.22 = f32[128,1024]{1,0:T(8,128)} copy(f32[128,1024]{1,0:T(8,128)S(1)} %get-tuple-element.138) | data formatting | bytes 1048576

commit v2 on v1

v2 whole, which is shorter than its diff:
```python
import functools
import itertools

import jax
import jax.numpy as jnp
from jax import lax
from jax.experimental import pallas as pl
from jax.experimental.pallas import tpu as pltpu
from jax.sharding import PartitionSpec as P

F32 = jnp.float32
BF16 = jnp.bfloat16
MESH = pl.DeviceIdType.MESH
SOFTEN = 0.01

TALL = 64
FILLS = (10, 20, 25, 48)
PARTS = 4
AWAY = (2, 3, 1, 0)


def split(value):
    high = value.astype(BF16)
    return high, (value - high.astype(F32)).astype(BF16)


def product(left, right_high, right_low):
    rows = left.shape[0] // 2
    both = jnp.dot(left, right_high, preferred_element_type=F32)
    rest = jnp.dot(left[:rows], right_low, preferred_element_type=F32)
    return both[:rows] + both[rows:] + rest


def stacked(value):
    return jnp.concatenate(split(value), axis=0)


def remote(source, target, sends, receives, device):
    return pltpu.make_async_remote_copy(
        src_ref=source,
        dst_ref=target,
        send_sem=sends,
        recv_sem=receives,
        device_id=device,
        device_id_type=MESH,
    )


def kernel(
    bits,
    sizes,
    x_hbm,
    points_hbm,
    mask_hbm,
    compress_hbm,
    self_hbm,
    partner_hbm,
    expand_hbm,
    out,
    mask,
    x,
    points,
    columns,
    spread,
    compress,
    weights,
    weights_high,
    weights_low,
    expand,
    expand_high,
    expand_low,
    g_high,
    g_low,
    x_both,
    near,
    state,
    moved,
    peer_state,
    share,
    first,
    straight,
    relayed,
    load_sem,
    expand_sem,
    sent_sems,
    level_sems,
    peer_sems,
    peer_expand_sems,
    points_sems,
    x_sems,
    first_sems,
    straight_sem,
    relayed_sems,
):
    n_grp, n_node = sizes
    levels = len(bits)
    cols, block = x_hbm.shape
    rank = compress_hbm.shape[1]
    part = cols // PARTS
    half = block // 2
    ring = n_grp // 2

    grp, node = lax.axis_index("grp"), lax.axis_index("node")
    y, core = lax.div(grp, 2), lax.rem(grp, 2)

    def along(step):
        return (lax.rem(y + step, ring) * 2 + core, node)

    up, down = along(1), along(ring - 1)
    peer = (grp + 1 - 2 * core, node)
    after, before = (grp, node + 1), (grp, node - 1)

    def partner(bit):
        apart = 1 << bit
        return (grp, node + apart * (1 - 2 * lax.rem(lax.div(node, apart), 2)))

    partners = [partner(bit) for bit in bits]
    has_before, has_after = node > 0, node < n_node - 1

    loads = [
        pltpu.make_async_copy(x_hbm, x.at[0], load_sem.at[0]),
        pltpu.make_async_copy(compress_hbm, compress, load_sem.at[1]),
        pltpu.make_async_copy(points_hbm, points.at[0], load_sem.at[2]),
        pltpu.make_async_copy(mask_hbm, mask, load_sem.at[3]),
        pltpu.make_async_copy(self_hbm, weights.at[0], load_sem.at[4]),
        pltpu.make_async_copy(partner_hbm, weights.at[1], load_sem.at[4]),
    ]
    for load in loads[:2]:
        load.start()

    barrier = pltpu.get_barrier_semaphore()

    def greet(device):
        pl.semaphore_signal(barrier, inc=1, device_id=device, device_id_type=MESH)

    everyone = partners + [peer, up, down]
    for device in everyone:
        greet(device)

    @pl.when(has_before)
    def _():
        greet(before)

    @pl.when(has_after)
    def _():
        greet(after)

    for load in loads[2:]:
        load.start()

    def expand_columns(slot, of_core):
        target = lax.rem(y + AWAY[slot], ring) * 2 + of_core
        return expand_hbm.at[:, pl.ds(pl.multiple_of(target * block, block), block)]

    own_expand = [
        pltpu.make_async_copy(expand_columns(slot, core), expand.at[slot, pl.ds(0, rank)], expand_sem)
        for slot in range(ring)
    ]

    with jax.named_scope("load_x"):
        loads[0].wait()
    with jax.named_scope("split_x"):
        x_both[0] = stacked(x[0])
    with jax.named_scope("load_c"):
        loads[1].wait()
        for copy in own_expand:
            copy.start()
    with jax.named_scope("compress"):
        state[0] = product(x_both[0], *split(compress[...]))

    with jax.named_scope("barrier"):
        pl.semaphore_wait(barrier, len(everyone) + has_before.astype(jnp.int32) + has_after.astype(jnp.int32))

    def level_copy(level, chunk):
        rows = pl.ds(pl.multiple_of(chunk * part, part), part)
        return remote(
            state.at[level, rows],
            moved.at[level, rows],
            sent_sems.at[level],
            level_sems.at[level, chunk],
            partners[level],
        )

    for chunk in range(PARTS):
        level_copy(0, chunk).start()

    loads[2].wait()
    to_after = remote(points.at[0], points.at[1], points_sems.at[0, 0], points_sems.at[1, 0], after)
    to_before = remote(points.at[0], points.at[2], points_sems.at[0, 1], points_sems.at[1, 1], before)

    @pl.when(has_after)
    def _():
        to_after.start()

    @pl.when(has_before)
    def _():
        to_before.start()

    @pl.when(jnp.logical_not(has_before))
    def _():
        points[1] = jnp.zeros_like(points[1])
        x[1] = jnp.zeros_like(x[1])

    @pl.when(jnp.logical_not(has_after))
    def _():
        points[2] = jnp.zeros_like(points[2])
        x[2] = jnp.zeros_like(x[2])

    peer_expand = [
        remote(
            expand_columns(slot, 1 - core),
            expand.at[slot, pl.ds(rank, rank)],
            peer_expand_sems.at[0],
            peer_expand_sems.at[1],
            peer,
        )
        for slot in range(ring)
    ]
    for copy in peer_expand:
        copy.start()

    with jax.named_scope("split_w"):
        loads[3].wait()
        pltpu.make_async_copy(weights, weights, load_sem.at[4]).wait()
        for level in range(levels):
            for which in range(2):
                high, low = split(weights[which, level])
                weights_high[which, level] = high
                weights_low[which, level] = low

    def turn(which):
        padded = jnp.concatenate([points[which] * 32.0, jnp.zeros((5, block), F32)], axis=0)
        columns[pl.ds(which * block, block), :] = padded.T

    def g_rows(index):
        for piece in range(TALL // 16):
            rows = pl.ds(pl.multiple_of(index * TALL + piece * 16, 16), 16)
            column = columns[rows, :]
            for side in range(2):
                span = pl.ds(side * half, half)
                total = None
                for axis in range(3):
                    source = jnp.broadcast_to(column[:, axis : axis + 1], (16, half))
                    target = jnp.concatenate([spread[axis, :, span]] * 2, axis=0)
                    apart = source - target
                    total = apart * apart if total is None else total + apart * apart
                high, low = split(lax.rsqrt(total + SOFTEN * 1024.0))
                g_high[rows, span] = high
                g_low[rows, span] = low

    wide = block // TALL

    def g_span(low, high):
        def body(index, carry):
            g_rows(index)
            return carry

        lax.fori_loop(low, high, body, 0)

    def near_part(which):
        def near_body(index, carry):
            span = pl.ds(pl.multiple_of(index * 512, 512), 512)
            rows = pl.ds(which * block, block)
            term = product(x_both[which], g_high[rows, span], g_low[rows, span])
            near[:, span] = term if which == 0 else near[:, span] + term
            return carry

        with jax.named_scope(f"near{which}"):
            lax.fori_loop(0, block // 512, near_body, 0)

    with jax.named_scope("turn0"):
        for axis in range(3):
            spread[axis] = jnp.broadcast_to(points[0, axis : axis + 1, :] * 32.0, (8, block))
        turn(0)
    with jax.named_scope("g_own"):
        g_span(0, FILLS[0])

    def level_step(level, chunk):
        rows = pl.ds(pl.multiple_of(chunk * part, part), part)
        with jax.named_scope(f"own{level}"):
            own = product(stacked(state[level, rows]), weights_high[0, level], weights_low[0, level])
        with jax.named_scope(f"wait{level}"):
            level_copy(level, chunk).wait_recv()
        with jax.named_scope(f"came{level}"):
            came = product(stacked(moved[level, rows]), weights_high[1, level], weights_low[1, level])
            state[level + 1, rows] = own + came

    for level in range(levels - 1):

        def level_body(chunk, carry, level=level):
            level_step(level, chunk)
            level_copy(level + 1, chunk).start()
            return carry

        lax.fori_loop(0, PARTS, level_body, 0)
        if level == 0:
            with jax.named_scope("turn12"):
                pl.when(has_before)(to_after.wait_recv)
                pl.when(has_after)(to_before.wait_recv)
                turn(1)
                turn(2)
            with jax.named_scope("g_1"):
                g_span(FILLS[0], FILLS[1])

    x_after = remote(x.at[0], x.at[1], x_sems.at[0, 0], x_sems.at[1, 0], after)
    x_before = remote(x.at[0], x.at[2], x_sems.at[0, 1], x_sems.at[1, 1], before)
    pl.when(has_after)(x_after.start)
    pl.when(has_before)(x_before.start)

    whole_expand = remote(
        expand.at[:, pl.ds(0, rank)],
        expand.at[:, pl.ds(rank, rank)],
        peer_expand_sems.at[0],
        peer_expand_sems.at[1],
        peer,
    )
    with jax.named_scope("wait_e"):
        pltpu.make_async_copy(
            expand.at[:, pl.ds(0, rank)], expand.at[:, pl.ds(0, rank)], expand_sem
        ).wait()
        whole_expand.wait_recv()
    for slot in range(ring):

        def convert(index, carry, slot=slot):
            rows = pl.ds(pl.multiple_of(index * 32, 32), 32)
            high, low = split(expand[slot, rows, :])
            expand_high[slot, rows, :] = high
            expand_low[slot, rows, :] = low
            return carry

        with jax.named_scope("convert"):
            lax.fori_loop(0, rank // 16, convert, 0)

    with jax.named_scope("g_2"):
        g_span(FILLS[1], FILLS[2])

    def peer_copy(chunk):
        rows = pl.ds(pl.multiple_of(chunk * part, part), part)
        return remote(
            state.at[levels, rows],
            peer_state.at[rows],
            sent_sems.at[levels],
            peer_sems.at[chunk],
            peer,
        )

    def first_copy(chunk, side):
        return remote(
            share.at[chunk, 0, side],
            first.at[chunk, side],
            sent_sems.at[levels + 1],
            first_sems.at[chunk, side],
            (down, up)[side],
        )

    def straight_copy(chunk, side):
        return remote(
            share.at[chunk, 1 + side, 1 - side],
            straight.at[chunk, side],
            sent_sems.at[levels + 1],
            straight_sem,
            (down, up)[side],
        )

    def relayed_copy(chunk, side):
        return remote(
            share.at[chunk, 1 + side, side],
            relayed.at[chunk, side],
            sent_sems.at[levels + 1],
            relayed_sems.at[chunk, side],
            (down, up)[side],
        )

    def far_step(chunk):
        rows = pl.ds(pl.multiple_of(chunk * part, part), part)
        with jax.named_scope("wait_peer"):
            peer_copy(chunk).wait_recv()
        both = jnp.concatenate([stacked(state[levels, rows]), stacked(peer_state[rows])], axis=1)
        for slot in range(ring):
            with jax.named_scope(f"far{slot}"):
                value = product(both, expand_high[slot], expand_low[slot])
                share[chunk, slot, 0] = value[:, :half]
                share[chunk, slot, 1] = value[:, half:]
            if slot == 0:
                first_copy(chunk, 0).start()
                first_copy(chunk, 1).start()
            if slot == 1:
                straight_copy(chunk, 0).start()
            if slot == 2:
                straight_copy(chunk, 1).start()

    def relay_step(chunk):
        for side in range(2):
            with jax.named_scope("wait_first"):
                first_copy(chunk, side).wait_recv()
            share[chunk, 1 + side, side] = share[chunk, 1 + side, side] + first[chunk, side]
            relayed_copy(chunk, side).start()

    def near_ready(which):
        with jax.named_scope(f"wait_x{which}"):
            if which == 1:
                pl.when(has_before)(x_after.wait_recv)
            else:
                pl.when(has_after)(x_before.wait_recv)
        x_both[which] = stacked(x[which] * mask[0, which - 1].astype(F32))
        near_part(which)

    def main_body(step, carry):
        @pl.when(step < PARTS)
        def _():
            level_step(levels - 1, step)
            peer_copy(step).start()

        @pl.when(step >= 1)
        def _():
            far_step(step - 1)

        return carry

    lax.fori_loop(0, PARTS + 1, main_body, 0)

    relay_step(0)
    with jax.named_scope("g_fill"):
        g_span(FILLS[2], FILLS[3])
    relay_step(1)
    near_part(0)
    relay_step(2)
    near_ready(1)
    relay_step(3)
    near_ready(2)

    def final_body(chunk, carry):
        rows = pl.ds(pl.multiple_of(chunk * part, part), part)
        for side in range(2):
            with jax.named_scope("wait_relayed"):
                relayed_copy(chunk, side).wait_recv()
            span = pl.ds(side * half, half)
            out[rows, span] = (
                near[rows, span]
                + share[chunk, 3, side]
                + straight[chunk, 1 - side]
                + relayed[chunk, side]
            )
        return carry

    with jax.named_scope("wait_straight"):
        remote(straight, straight, sent_sems.at[levels + 1], straight_sem, up).wait_recv()
    lax.fori_loop(0, PARTS, final_body, 0)

    with jax.named_scope("drain"):
        for level in range(levels):
            remote(
                state.at[level], moved.at[level], sent_sems.at[level], level_sems.at[level, 0], up
            ).wait_send()
        remote(state.at[levels], peer_state, sent_sems.at[levels], peer_sems.at[0], up).wait_send()
        away = share.at[:, pl.ds(0, 3)]
        remote(away, away, sent_sems.at[levels + 1], straight_sem, up).wait_send()
        whole_expand.wait_send()
        for copy in (to_after, x_after):
            pl.when(has_after)(copy.wait_send)
        for copy in (to_before, x_before):
            pl.when(has_before)(copy.wait_send)


def order_kernel(order, number):
    number[0] = order[0] * 2 + (order[1] > order[2]).astype(jnp.int32)


def order_number(order):
    smem = pl.BlockSpec(memory_space=pltpu.SMEM)
    return pl.pallas_call(
        order_kernel,
        out_shape=jax.ShapeDtypeStruct((1,), jnp.int32),
        in_specs=[smem],
        out_specs=smem,
        name="order_number",
    )(order)


def solution(mesh):
    sizes = (mesh.shape["grp"], mesh.shape["node"])

    def shards(excitation, points, near_mask, bit_order, compress, level_self, level_partner, expand):
        cols, block = excitation.shape
        rank = compress.shape[1]
        levels = level_self.shape[0]
        part = cols // PARTS
        half = block // 2
        ring = sizes[0] // 2
        hbm = pl.BlockSpec(memory_space=pltpu.HBM)
        dma = pltpu.SemaphoreType.DMA

        def call(bits, number):
            return pl.pallas_call(
                functools.partial(kernel, bits, sizes),
                out_shape=jax.ShapeDtypeStruct((cols, block), F32),
                in_specs=[hbm] * 7,
                out_specs=pl.BlockSpec(memory_space=pltpu.VMEM),
                scratch_shapes=[
                    pltpu.SMEM((1, 2), jnp.int32),
                    pltpu.VMEM((3, cols, block), F32),
                    pltpu.VMEM((3, 3, block), F32),
                    pltpu.VMEM((3 * block, 8), F32),
                    pltpu.VMEM((3, 8, block), F32),
                    pltpu.VMEM((block, rank), F32),
                    pltpu.VMEM((2, levels, rank, rank), F32),
                    pltpu.VMEM((2, levels, rank, rank), BF16),
                    pltpu.VMEM((2, levels, rank, rank), BF16),
                    pltpu.VMEM((ring, 2 * rank, block), F32),
                    pltpu.VMEM((ring, 2 * rank, block), BF16),
                    pltpu.VMEM((ring, 2 * rank, block), BF16),
                    pltpu.VMEM((3 * block, block), BF16),
                    pltpu.VMEM((3 * block, block), BF16),
                    pltpu.VMEM((3, 2 * cols, block), BF16),
                    pltpu.VMEM((cols, block), F32),
                    pltpu.VMEM((levels + 1, cols, rank), F32),
                    pltpu.VMEM((levels, cols, rank), F32),
                    pltpu.VMEM((cols, rank), F32),
                    pltpu.VMEM((PARTS, ring, 2, part, half), F32),
                    pltpu.VMEM((PARTS, 2, part, half), F32),
                    pltpu.VMEM((PARTS, 2, part, half), F32),
                    pltpu.VMEM((PARTS, 2, part, half), F32),
                    dma((5,)),
                    dma,
                    dma((levels + 2,)),
                    dma((levels, PARTS)),
                    dma((PARTS,)),
                    dma((2,)),
                    dma((2, 2)),
                    dma((2, 2)),
                    dma((PARTS, 2)),
                    dma,
                    dma((PARTS, 2)),
                ],
                compiler_params=pltpu.CompilerParams(
                    collective_id=number, has_side_effects=True, vmem_limit_bytes=62 << 20
                ),
                name=f"far_near_{number}",
            )

        orders = list(itertools.permutations(range(levels)))
        branches = [call(bits, number) for number, bits in enumerate(orders)]
        return lax.switch(
            order_number(bit_order)[0],
            branches,
            excitation,
            points,
            near_mask,
            compress,
            level_self,
            level_partner,
            expand,
        )

    return jax.shard_map(
        shards,
        mesh=mesh,
        in_specs=(
            P(None, ("grp", "node")),
            P(None, ("grp", "node")),
            P(("grp", "node"), None),
            P(),
            P(("grp", "node"), None),
            P(None, ("grp", "node"), None),
            P(None, ("grp", "node"), None),
            P(("grp", "node"), None),
        ),
        out_specs=P(None, ("grp", "node")),
        check_vma=False,
    )
```

time: 58.5 us -> 42.4 us (0.72)
  the two profiles are of different devices: /device:TPU:2 before, /device:TPU:1 now
where the time goes in v2:
time: 42.4 us; the launch traced here: 42.3 us
  Pallas kernels  40.3 us (95%)
  local copies, waits for them, and re-layouts  0.8 us (2%)
  between operations  0.67 us (2%)
  loops' own time  0.57 us (1%)
    pallas_call x1, Pallas kernels, shards(): lax.switch(order_number(bit_order)[0], branches, excitation, points, near...  39.1 us
    pallas_call x1, Pallas kernels, order_number(): pl.pallas_call(order_kernel, out_shape=jax.ShapeDtypeStruct((1,), jnp.int...  1.18 us

profile of v2, /device:TPU:1, one launch (start us, length us, event | category | flops | bytes accessed | tf_op | source)
XLA Modules:
  0.0 42.3 jit_solution(12895851092769027397)
XLA Ops:
  0.0 1.2 %order_number.1 = s32[1]{0:T(128)} custom-call(s32[3]{0:T(128)} %order.1), custom_call_target="tpu_custom_call" | custom-call | tf_op jit(solution)/shard_map/order_number/pallas_call | solution.py:471
  1.8 39.6 %conditional.1 = (f32[128,1024]{1,0:T(8,128)S(1)}) conditional(s32[]{:T(128)} %bitcast, (f32[128,1024]{1,0:T(8,128)}, f32[3,1024]{1,0:T(4,128)}, s32[1,2]{1,0:T(1,128)}, f32[1024,256]{1,0:T(8,128)}, f32[3,256,256]{2,1,0:T(8,128)}, /*index=5*/f32[3,256,256]{2,1,0:T(8,128)}, f32[256,8192]{1,0:T(8,128)}) %tuple.23, ...), branch_computations={%region_0.0_spmd, %region_1.0_spmd, %region_2.0_spmd, %region_3.0_... | conditional | bytes 8 | solution.py:543
  2.1 39.1 %far_near_5.1 = f32[128,1024]{1,0:T(8,128)S(1)} custom-call(f32[128,1024]{1,0:T(8,128)} %get-tuple-element.131.x_hbm, f32[3,1024]{1,0:T(4,128)} %get-tuple-element.132.points_hbm, s32[1,2]{1,0:T(1,128)} %get-tuple-element.133.mask_hbm, f32[1024,256]{1,0:T(8,128)} %get-tuple-element.134.compress_hbm, f32[3,256,256]{2,1,0:T(8,128)} %get-tuple-element.135.self_hbm, ...), custom_call_target="tpu_custom_call" | custom-call | tf_op jit(solution)/shard_map/cond/branch_5_fun/far_near_5/pallas_call | solution.py:543
  41.5 0.8 %copy.22 = f32[128,1024]{1,0:T(8,128)} copy(f32[128,1024]{1,0:T(8,128)S(1)} %get-tuple-element.138) | data formatting | bytes 1048576

commit v3 on v2

--- a/solution.py
+++ b/solution.py
@@ -14,7 +14,9 @@
 SOFTEN = 0.01
 
 TALL = 64
-FILLS = (10, 20, 25, 48)
+AHEAD = 12
+FILLS = (10, 20, 25, 38, 48)
+PIECES = 2
 PARTS = 4
 AWAY = (2, 3, 1, 0)
 
@@ -81,6 +83,7 @@
     straight,
     relayed,
     load_sem,
+    first_sem,
     expand_sem,
     sent_sems,
     level_sems,
@@ -117,17 +120,27 @@
     partners = [partner(bit) for bit in bits]
     has_before, has_after = node > 0, node < n_node - 1
 
+    deep = block // PIECES
+
+    def depth(piece):
+        return pl.ds(piece * deep, deep)
+
+    first_loads = [
+        (
+            pltpu.make_async_copy(x_hbm.at[:, depth(piece)], x.at[0, :, depth(piece)], first_sem.at[piece]),
+            pltpu.make_async_copy(compress_hbm.at[depth(piece)], compress.at[depth(piece)], first_sem.at[PIECES + piece]),
+        )
+        for piece in range(PIECES)
+    ]
+    for pair in first_loads:
+        for load in pair:
+            load.start()
     loads = [
-        pltpu.make_async_copy(x_hbm, x.at[0], load_sem.at[0]),
-        pltpu.make_async_copy(compress_hbm, compress, load_sem.at[1]),
-        pltpu.make_async_copy(points_hbm, points.at[0], load_sem.at[2]),
-        pltpu.make_async_copy(mask_hbm, mask, load_sem.at[3]),
-        pltpu.make_async_copy(self_hbm, weights.at[0], load_sem.at[4]),
-        pltpu.make_async_copy(partner_hbm, weights.at[1], load_sem.at[4]),
+        pltpu.make_async_copy(points_hbm, points.at[0], load_sem.at[0]),
+        pltpu.make_async_copy(mask_hbm, mask, load_sem.at[1]),
+        pltpu.make_async_copy(self_hbm, weights.at[0], load_sem.at[2]),
+        pltpu.make_async_copy(partner_hbm, weights.at[1], load_sem.at[2]),
     ]
-    for load in loads[:2]:
-        load.start()
-
     barrier = pltpu.get_barrier_semaphore()
 
     def greet(device):
@@ -145,8 +158,6 @@
     def _():
         greet(after)
 
-    for load in loads[2:]:
-        load.start()
 
     def expand_columns(slot, of_core):
         target = lax.rem(y + AWAY[slot], ring) * 2 + of_core
@@ -157,16 +168,22 @@
         for slot in range(ring)
     ]
 
-    with jax.named_scope("load_x"):
-        loads[0].wait()
-    with jax.named_scope("split_x"):
-        x_both[0] = stacked(x[0])
-    with jax.named_scope("load_c"):
-        loads[1].wait()
-        for copy in own_expand:
-            copy.start()
-    with jax.named_scope("compress"):
-        state[0] = product(x_both[0], *split(compress[...]))
+    total = None
+    for piece in range(PIECES):
+        with jax.named_scope("load_x"):
+            for load in first_loads[piece]:
+                load.wait()
+        if piece == 0:
+            for load in loads:
+                load.start()
+        with jax.named_scope("compress"):
+            value = stacked(x[0, :, depth(piece)])
+            x_both[0, :, depth(piece)] = value
+            value = product(value, *split(compress[depth(piece), :]))
+            total = value if total is None else total + value
+    state[0] = total
+    for copy in own_expand:
+        copy.start()
 
     with jax.named_scope("barrier"):
         pl.semaphore_wait(barrier, len(everyone) + has_before.astype(jnp.int32) + has_after.astype(jnp.int32))
@@ -184,7 +201,7 @@
     for chunk in range(PARTS):
         level_copy(0, chunk).start()
 
-    loads[2].wait()
+    loads[0].wait()
     to_after = remote(points.at[0], points.at[1], points_sems.at[0, 0], points_sems.at[1, 0], after)
     to_before = remote(points.at[0], points.at[2], points_sems.at[0, 1], points_sems.at[1, 1], before)
 
@@ -220,8 +237,8 @@
         copy.start()
 
     with jax.named_scope("split_w"):
-        loads[3].wait()
-        pltpu.make_async_copy(weights, weights, load_sem.at[4]).wait()
+        loads[1].wait()
+        pltpu.make_async_copy(weights, weights, load_sem.at[2]).wait()
         for level in range(levels):
             for which in range(2):
                 high, low = split(weights[which, level])
@@ -349,7 +366,7 @@
             share.at[chunk, 0, side],
             first.at[chunk, side],
             sent_sems.at[levels + 1],
-            first_sems.at[chunk, side],
+            first_sems.at[chunk],
             (down, up)[side],
         )
 
@@ -367,7 +384,7 @@
             share.at[chunk, 1 + side, side],
             relayed.at[chunk, side],
             sent_sems.at[levels + 1],
-            relayed_sems.at[chunk, side],
+            relayed_sems.at[chunk],
             (down, up)[side],
         )
 
@@ -376,23 +393,34 @@
         with jax.named_scope("wait_peer"):
             peer_copy(chunk).wait_recv()
         both = jnp.concatenate([stacked(state[levels, rows]), stacked(peer_state[rows])], axis=1)
-        for slot in range(ring):
-            with jax.named_scope(f"far{slot}"):
+        def far_slot(slot, carry):
+            with jax.named_scope("far"):
                 value = product(both, expand_high[slot], expand_low[slot])
                 share[chunk, slot, 0] = value[:, :half]
                 share[chunk, slot, 1] = value[:, half:]
-            if slot == 0:
+
+            @pl.when(slot == 0)
+            def _():
                 first_copy(chunk, 0).start()
                 first_copy(chunk, 1).start()
-            if slot == 1:
+
+            @pl.when(slot == 1)
+            def _():
                 straight_copy(chunk, 0).start()
-            if slot == 2:
+
+            @pl.when(slot == 2)
+            def _():
                 straight_copy(chunk, 1).start()
 
+            return carry
+
+        lax.fori_loop(0, ring, far_slot, 0)
+
     def relay_step(chunk):
+        with jax.named_scope("wait_first"):
+            both = first.at[chunk]
+            remote(both, both, sent_sems.at[levels + 1], first_sems.at[chunk], up).wait_recv()
         for side in range(2):
-            with jax.named_scope("wait_first"):
-                first_copy(chunk, side).wait_recv()
             share[chunk, 1 + side, side] = share[chunk, 1 + side, side] + first[chunk, side]
             relayed_copy(chunk, side).start()
 
@@ -405,35 +433,46 @@
         x_both[which] = stacked(x[which] * mask[0, which - 1].astype(F32))
         near_part(which)
 
-    def main_body(step, carry):
-        @pl.when(step < PARTS)
+    def last_level(chunk, carry=0):
+        level_step(levels - 1, chunk)
+        peer_copy(chunk).start()
+        return carry
+
+    lax.fori_loop(0, 1 + (PARTS - 1) * core, last_level, 0)
+
+    begun = FILLS[2] + AHEAD * core
+    with jax.named_scope("g_ahead"):
+        g_span(FILLS[2], begun)
+
+    def main_body(chunk, carry):
+        far_step(chunk)
+
+        @pl.when(jnp.logical_and(core == 0, chunk < PARTS - 1))
         def _():
-            level_step(levels - 1, step)
-            peer_copy(step).start()
-
-        @pl.when(step >= 1)
-        def _():
-            far_step(step - 1)
+            last_level(chunk + 1)
 
         return carry
 
-    lax.fori_loop(0, PARTS + 1, main_body, 0)
+    lax.fori_loop(0, PARTS, main_body, 0)
 
     relay_step(0)
     with jax.named_scope("g_fill"):
-        g_span(FILLS[2], FILLS[3])
+        g_span(begun, FILLS[3])
     relay_step(1)
+    with jax.named_scope("g_fill"):
+        g_span(FILLS[3], FILLS[4])
+    relay_step(2)
     near_part(0)
-    relay_step(2)
+    relay_step(3)
     near_ready(1)
-    relay_step(3)
     near_ready(2)
 
     def final_body(chunk, carry):
         rows = pl.ds(pl.multiple_of(chunk * part, part), part)
+        with jax.named_scope("wait_relayed"):
+            both = relayed.at[chunk]
+            remote(both, both, sent_sems.at[levels + 1], relayed_sems.at[chunk], up).wait_recv()
         for side in range(2):
-            with jax.named_scope("wait_relayed"):
-                relayed_copy(chunk, side).wait_recv()
             span = pl.ds(side * half, half)
             out[rows, span] = (
                 near[rows, span]
@@ -520,7 +559,8 @@
                     pltpu.VMEM((PARTS, 2, part, half), F32),
                     pltpu.VMEM((PARTS, 2, part, half), F32),
                     pltpu.VMEM((PARTS, 2, part, half), F32),
-                    dma((5,)),
+                    dma((3,)),
+                    dma((2 * PIECES,)),
                     dma,
                     dma((levels + 2,)),
                     dma((levels, PARTS)),
@@ -528,9 +568,9 @@
                     dma((2,)),
                     dma((2, 2)),
                     dma((2, 2)),
-                    dma((PARTS, 2)),
+                    dma((PARTS,)),
                     dma,
-                    dma((PARTS, 2)),
+                    dma((PARTS,)),
                 ],
                 compiler_params=pltpu.CompilerParams(
                     collective_id=number, has_side_effects=True, vmem_limit_bytes=62 << 20

time: 42.4 us -> 42.3 us (level)
  no operation moved by 1% of the time
where the time goes in v3:
time: 42.3 us; the launch traced here: 42.2 us
  Pallas kernels  40.5 us (96%)
  local copies, waits for them, and re-layouts  0.8 us (2%)
  between operations  0.67 us (2%)
    pallas_call x1, Pallas kernels, shards(): lax.switch(order_number(bit_order)[0], branches, excitation, points, near...  39.3 us
    pallas_call x1, Pallas kernels, order_number(): pl.pallas_call(order_kernel, out_shape=jax.ShapeDtypeStruct((1,), jnp.int...  1.18 us

profile of v3, /device:TPU:1, one launch (start us, length us, event | category | flops | bytes accessed | tf_op | source)
XLA Modules:
  0.0 42.2 jit_solution(17276329247309012702)
XLA Ops:
  0.0 1.2 %order_number.1 = s32[1]{0:T(128)} custom-call(s32[3]{0:T(128)} %order.1), custom_call_target="tpu_custom_call" | custom-call | tf_op jit(solution)/shard_map/order_number/pallas_call | solution.py:510
  1.8 39.5 %conditional.1 = (f32[128,1024]{1,0:T(8,128)S(1)}) conditional(s32[]{:T(128)} %bitcast, (f32[128,1024]{1,0:T(8,128)}, f32[3,1024]{1,0:T(4,128)}, s32[1,2]{1,0:T(1,128)}, f32[1024,256]{1,0:T(8,128)}, f32[3,256,256]{2,1,0:T(8,128)}, /*index=5*/f32[3,256,256]{2,1,0:T(8,128)}, f32[256,8192]{1,0:T(8,128)}) %tuple.23, ...), branch_computations={%region_0.0_spmd, %region_1.0_spmd, %region_2.0_spmd, %region_3.0_... | conditional | bytes 8 | solution.py:583
  1.9 39.3 %far_near_2.1 = f32[128,1024]{1,0:T(8,128)S(1)} custom-call(f32[128,1024]{1,0:T(8,128)} %get-tuple-element.110.x_hbm, f32[3,1024]{1,0:T(4,128)} %get-tuple-element.111.points_hbm, s32[1,2]{1,0:T(1,128)} %get-tuple-element.112.mask_hbm, f32[1024,256]{1,0:T(8,128)} %get-tuple-element.113.compress_hbm, f32[3,256,256]{2,1,0:T(8,128)} %get-tuple-element.114.self_hbm, ...), custom_call_target="tpu_custom_call" | custom-call | tf_op jit(solution)/shard_map/cond/branch_2_fun/far_near_2/pallas_call | solution.py:583
  41.4 0.8 %copy.22 = f32[128,1024]{1,0:T(8,128)} copy(f32[128,1024]{1,0:T(8,128)S(1)} %get-tuple-element.138) | data formatting | bytes 1048576
